TPU v7x, 32 devices: a whole 2x2x4 slice. The times are simulated.
32 devices in a mesh: occ: 4 (over y, x), vir: 8 (over z, core).
Axes of the slice: x: 2, y: 2, z: 4, core: 2. Of those that a mesh axis runs over, the one named last changes fastest.
Arguments:
- b_factors: float32 [32, 256, 4096], P('occ', 'vir'), may hold values from -0.6 to 0.6
- occ_energy: float32 [32], replicated, may hold values from -2 to -0.3
- vir_energy: float32 [256], replicated, may hold values from 0.2 to 3
Outputs:
- gamma: float32 [32, 256, 4096], P('occ', 'vir')
All inputs are finite; a program needn't handle non-finite values.
Results may differ from a plain program's by a relative error of at most 0.0003.
Values sent between devices are 32-bit elements; how exact they have to be, the bound alone decides.
A program may use at most 128 MiB of HBM per device.

v0:
```python
import jax
import jax.numpy as jnp
from jax import lax
from jax.sharding import PartitionSpec as P


def shifted(block, axis, distance):
    devices = range(lax.axis_size(axis))
    route = [((i - distance) % len(devices), i) for i in devices]
    return lax.ppermute(block, axis, route)


def local(b_factors, occ_energy, vir_energy):
    occ_block, vir_block, width = b_factors.shape
    occ_count = lax.axis_size("occ")
    vir_count = lax.axis_size("vir")
    occ_here = lax.axis_index("occ")
    vir_here = lax.axis_index("vir")
    high = lax.Precision.HIGHEST

    def gap_of(occ_place, vir_place):
        occ_part = lax.dynamic_slice_in_dim(
            occ_energy, occ_place % occ_count * occ_block, occ_block
        )
        vir_part = lax.dynamic_slice_in_dim(
            vir_energy, vir_place % vir_count * vir_block, vir_block
        )
        return (occ_part[:, None] - vir_part[None, :]).reshape(-1)

    mine = b_factors.reshape(occ_block * vir_block, width)
    mine_gap = gap_of(occ_here, vir_here)

    def amplitude_with(other, other_gap):
        integral = jnp.dot(mine, other.T, precision=high, preferred_element_type=jnp.float32)
        return integral / (mine_gap[:, None] + other_gap[None, :])

    def contribute(other_block, other_gap):
        other = other_block.reshape(occ_block * vir_block, width)
        amplitude = amplitude_with(other, other_gap)
        return jnp.dot(amplitude, other, precision=high, preferred_element_type=jnp.float32)

    total = contribute(b_factors, mine_gap)
    occ_after = shifted(b_factors, "occ", -1)
    occ_before = shifted(b_factors, "occ", 1)
    vir_after = shifted(b_factors, "vir", -1)
    vir_before = shifted(b_factors, "vir", 1)
    occ_pair = [
        (occ_after, gap_of(occ_here + 1, vir_here)),
        (occ_before, gap_of(occ_here + occ_count - 1, vir_here)),
    ]
    vir_pair = [
        (vir_after, gap_of(occ_here, vir_here + 1)),
        (vir_before, gap_of(occ_here, vir_here + vir_count - 1)),
    ]
    visits = occ_pair + vir_pair
    for other_block, other_gap in visits:
        total = total + contribute(other_block, other_gap)
    return total.reshape(occ_block, vir_block, width)


def solution(mesh):
    in_specs = (P("occ", "vir", None), P(), P())
    out_specs = P("occ", "vir", None)
    return jax.shard_map(local, mesh=mesh, in_specs=in_specs, out_specs=out_specs, check_vma=False)
```

profile of v0, /device:TPU:0, one launch (start us, length us, event | category | flops | bytes accessed | tf_op | source)
XLA Modules:
  0.0 201.5 jit_solution(129164381712892398)
XLA Ops:
  0.0 0.5 collective-permute-start.3
  0.5 4.0 %collective-permute-start.2 = (f32[8,32,4096]{2,1,0:T(8,128)}, f32[8,32,4096]{2,1,0:T(8,128)}, u32[]{:S(2)}, u32[]{:S(2)}) collective-permute-start(f32[8,32,4096]{2,1,0:T(8,128)} %param.3), channel_id=1, source_target_pairs={{1,0},{2,1},{3,2},{4,3},{5,4},{6,5},{7,6},{0,7},{9,8},{10,9},{11,1... | collective-permute-start | bytes 12582920 | tf_op jit(solution)/shard_map/ppermute | solution.py:10
  4.5 2.9 %collective-permute-start = (f32[8,32,4096]{2,1,0:T(8,128)}, f32[8,32,4096]{2,1,0:T(8,128)}, u32[]{:S(2)}, u32[]{:S(2)}) collective-permute-start(f32[8,32,4096]{2,1,0:T(8,128)} %param.3), channel_id=1, source_target_pairs={{8,0},{16,8},{24,16},{0,24},{9,1},{17,9},{25,17},{1,25},{10,2},{18... | collective-permute-start | bytes 12582920 | tf_op jit(solution)/shard_map/ppermute | solution.py:10
  7.5 0.0 collective-permute-start.1
  7.5 0.8 fusion.3
  8.3 0.9 fusion.2
  9.2 0.1 broadcast_subtract_fusion.2
  9.3 0.1 sub.119
  9.3 0.1 sub.105
  9.4 0.1 sub.115
  9.5 0.1 sub.108
  9.6 0.1 sub.112
  9.6 0.0 copy-start
  9.6 12.0 %convolution_divide_fusion.4 = f32[256,256]{1,0:T(8,128)S(1)} fusion(f32[256,4096]{1,0:T(8,128)} %bitcast.26, f32[256]{0:T(256)S(1)} %sub.105), kind=kOutput, calls=%fused_computation.8 | convolution fusion | flops 3221356544 | bytes 4457472 | tf_op jit(solution)/shard_map/dot_general | solution.py:34
  21.7 0.0 copy-done
  21.7 3.8 %fusion.4 = f32[256,4096]{1,0:T(8,128)S(1)} fusion(f32[256,256]{1,0:T(8,128)S(1)} %convolution_divide_fusion.4, f32[256,4096]{1,0:T(8,128)S(1)} %bitcast.27), kind=kOutput, calls=%fused_computation.16 | convolution fusion | flops 3221225472 | bytes 8650752 | tf_op jit(solution)/shard_map/dot_general | solution.py:40
  25.4 67.9 %collective-permute-done.3 = f32[8,32,4096]{2,1,0:T(8,128)} collective-permute-done((f32[8,32,4096]{2,1,0:T(8,128)}, f32[8,32,4096]{2,1,0:T(8,128)}, u32[]{:S(2)}, u32[]{:S(2)}) %collective-permute-start.3) | collective-permute-done | bytes 4194336 | tf_op jit(solution)/shard_map/ppermute | solution.py:10
  93.4 5.7 %convolution_divide_fusion = f32[256,256]{1,0:T(8,128)S(1)} fusion(f32[256,4096]{1,0:T(8,128)S(1)} %bitcast.28, f32[256,4096]{1,0:T(8,128)} %bitcast.4, f32[256]{0:T(256)S(1)} %sub.119, f32[256]{0:T(256)S(1)} %sub.105), kind=kOutput, calls=%fused_computation.4 | convolution fusion | flops 3221356544 | bytes 8652800 | tf_op jit(solution)/shard_map/dot_general | solution.py:34
  99.1 5.6 %fusion.6 = f32[256,4096]{1,0:T(8,128)S(1)} fusion(f32[256,256]{1,0:T(8,128)S(1)} %convolution_divide_fusion, f32[256,4096]{1,0:T(8,128)} %bitcast.4), kind=kOutput, calls=%fused_computation.18 | convolution fusion | flops 3221225472 | bytes 8650752 | tf_op jit(solution)/shard_map/dot_general | solution.py:40
  104.7 0.0 collective-permute-done.2
  104.7 5.7 %convolution_divide_fusion.1 = f32[256,256]{1,0:T(8,128)S(1)} fusion(f32[256,4096]{1,0:T(8,128)S(1)} %bitcast.29, f32[256,4096]{1,0:T(8,128)} %bitcast.3, f32[256]{0:T(256)S(1)} %sub.115, f32[256]{0:T(256)S(1)} %sub.105), kind=kOutput, calls=%fused_computation.5 | convolution fusion | flops 3221356544 | bytes 8652800 | tf_op jit(solution)/shard_map/dot_general | solution.py:34
  110.5 5.4 %fusion.5 = f32[256,4096]{1,0:T(8,128)S(1)} fusion(f32[256,256]{1,0:T(8,128)S(1)} %convolution_divide_fusion.1, f32[256,4096]{1,0:T(8,128)} %bitcast.3), kind=kOutput, calls=%fused_computation.17 | convolution fusion | flops 3221225472 | bytes 8650752 | tf_op jit(solution)/shard_map/dot_general | solution.py:40
  115.9 0.0 collective-permute-done
  115.9 5.7 %convolution_divide_fusion.3 = f32[256,256]{1,0:T(8,128)S(1)} fusion(f32[256,4096]{1,0:T(8,128)S(1)} %bitcast.30, f32[256,4096]{1,0:T(8,128)} %bitcast.1, f32[256]{0:T(256)S(1)} %sub.108, f32[256]{0:T(256)S(1)} %sub.105), kind=kOutput, calls=%fused_computation.7 | convolution fusion | flops 3221356544 | bytes 8652800 | tf_op jit(solution)/shard_map/dot_general | solution.py:34
  121.6 5.8 %convolution_add_fusion.1 = f32[256,4096]{1,0:T(8,128)S(1)} fusion(f32[256,4096]{1,0:T(8,128)S(1)} %fusion.4, f32[256,256]{1,0:T(8,128)S(1)} %convolution_divide_fusion.3, f32[256,4096]{1,0:T(8,128)} %bitcast.1), kind=kOutput, calls=%fused_computation.2 | convolution fusion | flops 3222274048 | bytes 12845056 | tf_op jit(solution)/shard_map/dot_general | solution.py:40
  127.4 59.4 %collective-permute-done.1 = f32[8,32,4096]{2,1,0:T(8,128)} collective-permute-done((f32[8,32,4096]{2,1,0:T(8,128)}, f32[8,32,4096]{2,1,0:T(8,128)}, u32[]{:S(2)}, u32[]{:S(2)}) %collective-permute-start.1) | collective-permute-done | bytes 4194336 | tf_op jit(solution)/shard_map/ppermute | solution.py:10
  186.8 5.7 %convolution_divide_fusion.2 = f32[256,256]{1,0:T(8,128)S(1)} fusion(f32[256,4096]{1,0:T(8,128)S(1)} %bitcast.31, f32[256,4096]{1,0:T(8,128)} %bitcast.2, f32[256]{0:T(256)S(1)} %sub.112, f32[256]{0:T(256)S(1)} %sub.105), kind=kOutput, calls=%fused_computation.6 | convolution fusion | flops 3221356544 | bytes 8652800 | tf_op jit(solution)/shard_map/dot_general | solution.py:34
  192.5 9.0 %fusion.1 = f32[256,4096]{1,0:T(8,128)} fusion(f32[256,4096]{1,0:T(8,128)S(1)} %fusion.6, f32[256,4096]{1,0:T(8,128)S(1)} %fusion.5, f32[256,4096]{1,0:T(8,128)S(1)} %convolution_add_fusion.1, f32[256,256]{1,0:T(8,128)S(1)} %convolution_divide_fusion.2, f32[256,4096]{1,0:T(8,128)} %bitcast.2), kind=kOutput, calls=%fused_computation.3 | convolution fusion | flops 3224371200 | bytes 21233664 | tf_op jit(solution)/shard_map/dot_general | solution.py:40
Async XLA Ops:
  0.0 93.4 %collective-permute-start.3 = (f32[8,32,4096]{2,1,0:T(8,128)}, f32[8,32,4096]{2,1,0:T(8,128)}, u32[]{:S(2)}, u32[]{:S(2)}) collective-permute-start(f32[8,32,4096]{2,1,0:T(8,128)} %param.3), channel_id=1, source_target_pairs={{7,0},{0,1},{1,2},{2,3},{3,4},{4,5},{5,6},{6,7},{15,8},{8,9},{9,10... | collective-permute-start | bytes 12582920 | tf_op jit(solution)/shard_map/ppermute | solution.py:10
  0.5 104.2 %collective-permute-start.2 = (f32[8,32,4096]{2,1,0:T(8,128)}, f32[8,32,4096]{2,1,0:T(8,128)}, u32[]{:S(2)}, u32[]{:S(2)}) collective-permute-start(f32[8,32,4096]{2,1,0:T(8,128)} %param.3), channel_id=1, source_target_pairs={{1,0},{2,1},{3,2},{4,3},{5,4},{6,5},{7,6},{0,7},{9,8},{10,9},{11,1... | collective-permute-start | bytes 12582920 | tf_op jit(solution)/shard_map/ppermute | solution.py:10
  4.5 111.4 %collective-permute-start = (f32[8,32,4096]{2,1,0:T(8,128)}, f32[8,32,4096]{2,1,0:T(8,128)}, u32[]{:S(2)}, u32[]{:S(2)}) collective-permute-start(f32[8,32,4096]{2,1,0:T(8,128)} %param.3), channel_id=1, source_target_pairs={{8,0},{16,8},{24,16},{0,24},{9,1},{17,9},{25,17},{1,25},{10,2},{18... | collective-permute-start | bytes 12582920 | tf_op jit(solution)/shard_map/ppermute | solution.py:10
  7.5 179.3 %collective-permute-start.1 = (f32[8,32,4096]{2,1,0:T(8,128)}, f32[8,32,4096]{2,1,0:T(8,128)}, u32[]{:S(2)}, u32[]{:S(2)}) collective-permute-start(f32[8,32,4096]{2,1,0:T(8,128)} %param.3), channel_id=1, source_target_pairs={{24,0},{0,8},{8,16},{16,24},{25,1},{1,9},{9,17},{17,25},{26,2},{2,... | collective-permute-start | bytes 12582920 | tf_op jit(solution)/shard_map/ppermute | solution.py:10
  9.6 12.0 %copy-start = (f32[8,32,4096]{2,1,0:T(8,128)S(1)}, f32[8,32,4096]{2,1,0:T(8,128)}, u32[]{:S(2)}) copy-start(f32[8,32,4096]{2,1,0:T(8,128)} %param.3) | copy-start | bytes 12582916
where the time goes:
time: 202 us
  waiting for transfers between devices  127 us (63%)
  matrix products  64.5 us (32%)
  starting transfers between devices  7.47 us (4%)
  local copies, waits for them, and re-layouts  2.1 us (1%)
    ppermute x4, waiting for transfers between devices, shifted(): return lax.ppermute(block, axis, route)  127 us
    dot_general x5, matrix products, amplitude_with(): jnp.dot(mine, other.T, precision=high, preferred_element_type=jnp.float32)  34.9 us
    dot_general x5, matrix products, contribute(): jnp.dot(amplitude, other, precision=high, preferred_element_type=jnp.floa...  29.6 us
    ppermute x4, starting transfers between devices, shifted(): return lax.ppermute(block, axis, route)  7.47 us
  transfers between devices with their start and end apart: 4, of which 2 were waited for; matrix products, arithmetic and copies ran while one was open for 26% of the time, Pallas kernels for 0%

commit v1 on v0

v1 whole, which is shorter than its diff:
```python
import functools

import jax
import jax.numpy as jnp
from jax import lax
from jax.experimental import pallas as pl
from jax.experimental.pallas import tpu as pltpu
from jax.sharding import PartitionSpec as P

MESH = pl.DeviceIdType.MESH
CHUNK = 256
AHEAD = 4
LAG = 2
TILE = 512


def split(value):
    high = value.astype(jnp.bfloat16)
    low = (value - high.astype(jnp.float32)).astype(jnp.bfloat16)
    return high, low


def product(a, b, contract):
    dims = ((contract[:1], contract[1:]), ((), ()))
    dot = functools.partial(lax.dot_general, dimension_numbers=dims, preferred_element_type=jnp.float32)
    (a_high, a_low), (b_high, b_low) = a, b
    return dot(a_high, b_high) + (dot(a_high, b_low) + dot(a_low, b_high))


def kernel(
    occ_count, vir_count, occ_block, vir_block,
    occ_ref, vir_ref, b_ref, out_ref,
    own, near, far, up, down, own_high, own_low, total, sums,
    own_sem, out_sem, near_send, near_recv, far_send, far_recv, up_send, up_recv, down_send, down_recv,
):
    rows, width = b_ref.shape
    chunks = width // CHUNK
    tiles = width // TILE
    o = lax.axis_index("occ")
    v = lax.axis_index("vir")
    step = 1 - 2 * lax.rem(o, 2)
    partner = o + step
    relay_to = lax.rem(o + 2 * step + occ_count, occ_count)
    relay_from = lax.rem(o - 2 * step + occ_count, occ_count)
    across = lax.rem(o - step + occ_count, occ_count)
    v_up = lax.rem(v + 1, vir_count)
    v_down = lax.rem(v + vir_count - 1, vir_count)

    def cols(k, size=CHUNK):
        return pl.ds(pl.multiple_of(k * size, size), size)

    def load(k):
        return pltpu.make_async_copy(b_ref.at[:, cols(k)], own.at[:, cols(k)], own_sem.at[k])

    def near_copy(k):
        return pltpu.make_async_remote_copy(
            b_ref.at[:, cols(k)], near.at[:, cols(k)], near_send.at[k], near_recv.at[k],
            device_id=(partner, v), device_id_type=MESH)

    def far_copy(k):
        return pltpu.make_async_remote_copy(
            near.at[:, cols(k)], far.at[:, cols(k)], far_send.at[k], far_recv.at[k],
            device_id=(relay_to, v), device_id_type=MESH)

    def up_copy(k):
        return pltpu.make_async_remote_copy(
            b_ref.at[:, cols(k)], down.at[:, cols(k)], up_send.at[k], down_recv.at[k],
            device_id=(o, v_up), device_id_type=MESH)

    def down_copy(k):
        return pltpu.make_async_remote_copy(
            b_ref.at[:, cols(k)], up.at[:, cols(k)], down_send.at[k], up_recv.at[k],
            device_id=(o, v_down), device_id_type=MESH)

    def send(k):
        near_copy(k).start()
        up_copy(k).start()
        down_copy(k).start()

    def every(count, body, first=0):
        def run(k, carry):
            body(k)
            return carry
        lax.fori_loop(first, count, run, 0)

    barrier = pltpu.get_barrier_semaphore()
    for device in ((partner, v), (relay_to, v), (relay_from, v), (o, v_up), (o, v_down)):
        pl.semaphore_signal(barrier, inc=1, device_id=device, device_id_type=MESH)
    every(chunks, lambda k: load(k).start())
    pl.semaphore_wait(barrier, 5)
    every(AHEAD, send)

    lane = lax.broadcasted_iota(jnp.int32, (8, rows), 1)
    inner = lane
    for i in range(1, occ_block):
        inner = inner - jnp.where(lane >= i * vir_block, vir_block, 0)

    def gap_row(occ_place, vir_place):
        occ_part = jnp.zeros((8, rows), jnp.float32)
        vir_part = jnp.zeros((8, rows), jnp.float32)
        for i in range(occ_block):
            occ_part = jnp.where(lane >= i * vir_block, occ_ref[occ_place * occ_block + i], occ_part)
        for a in range(vir_block):
            vir_part = jnp.where(inner == a, vir_ref[vir_place * vir_block + a], vir_part)
        return jnp.broadcast_to((occ_part - vir_part)[:1], (rows, rows))

    mine_gap = gap_row(o, v).T

    def gather(slot, block, k):
        a = (own_high[:, cols(k)], own_low[:, cols(k)])
        sums[slot] += product(a, split(block[:, cols(k)]), (1, 1))

    def amplitude(slot, occ_place, vir_place):
        return split(sums[slot] / (mine_gap + gap_row(occ_place, vir_place)))

    def spread(amp, block, fresh=False, last=False):
        def tile(t):
            here = cols(t, TILE)
            part = product(amp, split(block[:, here]), (1, 0))
            total[:, here] = part if fresh else total[:, here] + part
            if last:
                pltpu.make_async_copy(total.at[:, here], out_ref.at[:, here], out_sem.at[t]).start()
        every(tiles, tile)

    sums[...] = jnp.zeros_like(sums)

    def own_chunk(k):
        load(k).wait()
        high, low = split(own[:, cols(k)])
        own_high[:, cols(k)] = high
        own_low[:, cols(k)] = low
        gather(0, own, k)

    every(chunks, own_chunk)
    spread(amplitude(0, o, v), own, fresh=True)

    def lagged(k):
        up_copy(k).wait_send()
        down_copy(k).wait_send()
        near_copy(k).wait_send()
        down_copy(k).wait_recv()
        gather(2, up, k)
        up_copy(k).wait_recv()
        gather(3, down, k)

    def lagged_far(k):
        far_copy(k).wait()
        gather(4, far, k)

    def arrive(k):
        near_copy(k).wait_recv()
        far_copy(k).start()

        @pl.when(k + AHEAD < chunks)
        def _():
            send(k + AHEAD)

        gather(1, near, k)

        @pl.when(k >= LAG)
        def _():
            lagged(k - LAG)
            lagged_far(k - LAG)

    every(chunks, arrive)
    spread(amplitude(1, partner, v), near)
    every(chunks, lagged, chunks - LAG)
    spread(amplitude(2, o, v_up), up)
    spread(amplitude(3, o, v_down), down)
    every(chunks, lagged_far, chunks - LAG)
    spread(amplitude(4, across, v), far, last=True)

    def stored(t):
        here = cols(t, TILE)
        pltpu.make_async_copy(total.at[:, here], out_ref.at[:, here], out_sem.at[t]).wait()

    every(tiles, stored)


def local(b_factors, occ_energy, vir_energy):
    occ_block, vir_block, width = b_factors.shape
    occ_count = lax.axis_size("occ")
    vir_count = lax.axis_size("vir")
    rows = occ_block * vir_block
    chunks, tiles = width // CHUNK, width // TILE
    block = pltpu.VMEM((rows, width), jnp.float32)
    half = pltpu.VMEM((rows, width), jnp.bfloat16)
    sems = [pltpu.SemaphoreType.DMA((count,)) for count in [chunks, tiles] + [chunks] * 8]
    out = pl.pallas_call(
        functools.partial(kernel, occ_count, vir_count, occ_block, vir_block),
        out_shape=jax.ShapeDtypeStruct((rows, width), jnp.float32),
        in_specs=[
            pl.BlockSpec(memory_space=pltpu.SMEM),
            pl.BlockSpec(memory_space=pltpu.SMEM),
            pl.BlockSpec(memory_space=pl.ANY),
        ],
        out_specs=pl.BlockSpec(memory_space=pl.ANY),
        scratch_shapes=[block] * 5 + [half, half, block, pltpu.VMEM((5, rows, rows), jnp.float32)] + sems,
        compiler_params=pltpu.CompilerParams(
            collective_id=0, has_side_effects=True, vmem_limit_bytes=60 * 2**20),
    )(occ_energy, vir_energy, b_factors.reshape(rows, width))
    return out.reshape(occ_block, vir_block, width)


def solution(mesh):
    in_specs = (P("occ", "vir", None), P(), P())
    out_specs = P("occ", "vir", None)
    return jax.shard_map(local, mesh=mesh, in_specs=in_specs, out_specs=out_specs, check_vma=False)
```

time: 202 us -> 120 us (0.59)
  waiting for transfers between devices: 127 us -> 0 us
  Pallas kernels: 0 us -> 115 us
  matrix products: 64.5 us -> 0 us
  starting transfers between devices: 7.47 us -> 0 us
  local copies, waits for them, and re-layouts: 2.1 us -> 4.65 us
    ppermute x4 -> x0, waiting for transfers between devices: 127 us -> none  [shifted(): return lax.ppermute(block, axis, route)]
    pallas_call x0 -> x1, Pallas kernels: none -> 115 us  [local(): pl.pallas_call(functools.partial(kernel, occ_count, vir_count, occ_block,...]
    dot_general x10 -> x0, matrix products: 64.5 us -> none  [the longest x5 34.9 us: amplitude_with(): jnp.dot(mine, other.T, precision=high, preferred_element_type=jnp.float32)]
    ppermute x4 -> x0, starting transfers between devices: 7.47 us -> none  [shifted(): return lax.ppermute(block, axis, route)]
    unnamed x2 -> x1, local copies, waits for them, and re-layouts: 0.01 us -> 4.65 us
  transfers between devices with their start and end apart: 4 -> 0, of which waited for: 2 -> 0; matrix products, arithmetic and copies ran while one was open for 26% -> 0% of each run, Pallas kernels for 0% -> 0%
where the time goes in v1:
time: 120 us; the launch traced here: 119 us
  Pallas kernels  115 us (96%)
  local copies, waits for them, and re-layouts  4.65 us (4%)
    pallas_call x1, Pallas kernels, local(): pl.pallas_call(functools.partial(kernel, occ_count, vir_count, occ_block,...  115 us
    unnamed x1, local copies, waits for them, and re-layouts  4.65 us

profile of v1, /device:TPU:0, one launch (start us, length us, event | category | flops | bytes accessed | tf_op | source)
XLA Modules:
  0.0 119.3 jit_solution(651992365954540939)
XLA Ops:
  0.0 114.7 %shard_map.37 = f32[256,4096]{1,0:T(8,128)} custom-call(f32[32]{0:T(128)} %occ_ref.1, f32[256]{0:T(256)} %vir_ref.1, f32[256,4096]{1,0:T(8,128)} %bitcast.3), custom_call_target="tpu_custom_call" | custom-call | tf_op jit(solution)/shard_map/pallas_call | solution.py:189
  114.7 4.7 %copy.5 = f32[8,32,4096]{2,1,0:T(8,128)} copy(f32[8,32,4096]{2,1,0:T(8,128)} %bitcast.2) | data formatting | bytes 8388608

commit v2 on v1

v2 whole, which is shorter than its diff:
```python
import functools

import jax
import jax.numpy as jnp
from jax import lax
from jax.experimental import pallas as pl
from jax.experimental.pallas import tpu as pltpu
from jax.sharding import PartitionSpec as P

MESH = pl.DeviceIdType.MESH
CHUNK = 512
AHEAD = 4
LAG = 2
STREAMS = 4


def split(value):
    high = value.astype(jnp.bfloat16)
    low = (value - high.astype(jnp.float32)).astype(jnp.bfloat16)
    return high, low


def product(a, b, contract):
    dims = ((contract[:1], contract[1:]), ((), ()))
    dot = functools.partial(lax.dot_general, dimension_numbers=dims, preferred_element_type=jnp.float32)
    (a_high, a_low), (b_high, b_low) = a, b
    return dot(a_high, b_high) + (dot(a_high, b_low) + dot(a_low, b_high))


def cols(k):
    return pl.ds(pl.multiple_of(k * CHUNK, CHUNK), CHUNK)


def every(count, body, first=0):
    def run(k, carry):
        body(k)
        return carry
    lax.fori_loop(first, count, run, 0)


def kernel(
    occ_count, vir_count, occ_block, vir_block,
    occ_ref, vir_ref, b_ref, total, land, amp_high, amp_low,
    own, own_high, own_low, sums, mine_gap, vir_row,
    own_sem, near_send, near_recv, far_send, far_recv, inner_send, inner_recv, outer_send, outer_recv,
):
    rows, width = b_ref.shape
    piece = rows // STREAMS
    occ_piece = occ_block // STREAMS
    chunks = width // CHUNK
    steps = STREAMS * chunks
    o = lax.axis_index("occ")
    v = lax.axis_index("vir")
    step = 1 - 2 * lax.rem(o, 2)
    partner = o + step
    relay_to = lax.rem(o + 2 * step + occ_count, occ_count)
    relay_from = lax.rem(o - 2 * step + occ_count, occ_count)
    across = lax.rem(o - step + occ_count, occ_count)
    turn = 1 - 2 * lax.rem(v, 2)
    v_inner = v + turn
    v_outer = lax.rem(v - turn + vir_count, vir_count)
    sources = ((partner, v), (o, v_inner), (o, v_outer), (across, v))

    def sent(k):
        return b_ref.at[pl.ds(pl.multiple_of(k // chunks * piece, piece), piece), cols(k % chunks)]

    def landed(k, stream):
        return land.at[k // chunks, pl.ds(stream * piece, piece), cols(k % chunks)]

    def remote(k, source, stream, send_sem, recv_sem, device):
        return pltpu.make_async_remote_copy(
            source, landed(k, stream), send_sem.at[k], recv_sem.at[k], device_id=device, device_id_type=MESH)

    def load(k):
        return pltpu.make_async_copy(b_ref.at[:, cols(k)], own.at[:, cols(k)], own_sem.at[k])

    def near_copy(k):
        return remote(k, sent(k), 0, near_send, near_recv, (partner, v))

    def inner_copy(k):
        return remote(k, sent(k), 1, inner_send, inner_recv, (o, v_inner))

    def outer_copy(k):
        return remote(k, sent(k), 2, outer_send, outer_recv, (o, v_outer))

    def far_copy(k):
        return remote(k, landed(k, 0), 3, far_send, far_recv, (relay_to, v))

    def send(k):
        near_copy(k).start()
        outer_copy(k).start()
        inner_copy(k).start()

    barrier = pltpu.get_barrier_semaphore()
    for device in ((partner, v), (relay_to, v), (relay_from, v), (o, v_inner), (o, v_outer)):
        pl.semaphore_signal(barrier, inc=1, device_id=device, device_id_type=MESH)
    pl.semaphore_wait(barrier, 5)
    every(AHEAD, send)
    every(chunks, lambda k: load(k).start())

    lane = lax.broadcasted_iota(jnp.int32, (8, rows), 1)
    within = lane
    for i in range(1, occ_block):
        within = within - jnp.where(lane >= i * vir_block, vir_block, 0)

    def vir_values(blocks):
        values = jnp.zeros((8, rows), jnp.float32)
        for stream, block in enumerate(blocks):
            part = values
            for a in range(vir_block):
                part = jnp.where(within == a, vir_ref[block * vir_block + a], part)
            values = jnp.where(lane >= stream * piece, part, values)
        return values

    def occ_values(places):
        values = jnp.zeros((8, rows), jnp.float32)
        for i, place in enumerate(places):
            values = jnp.where(lane >= i * vir_block, occ_ref[place], values)
        return values

    def whole(row):
        return jnp.broadcast_to(row[:1], (rows, rows))

    own_row = occ_values([o * occ_block + i for i in range(occ_block)]) - vir_values([v])
    mine_gap[...] = whole(own_row).T
    vir_row[...] = vir_values([block for _, block in sources])

    def gather(block, k):
        a = (own_high[:, cols(k)], own_low[:, cols(k)])
        sums[...] += product(a, split(block), (1, 1))

    def amplitude(row):
        amp_high[...], amp_low[...] = split(sums[...] / (mine_gap[...] + whole(row)))
        sums[...] = jnp.zeros_like(sums)

    def spread(block):
        return product((amp_high[...], amp_low[...]), split(block), (1, 0))

    sums[...] = jnp.zeros_like(sums)

    def own_chunk(k):
        load(k).wait()
        high, low = split(own[:, cols(k)])
        own_high[:, cols(k)] = high
        own_low[:, cols(k)] = low
        gather(own[:, cols(k)], k)

    every(chunks, own_chunk)
    amplitude(own_row)

    def own_spread(k):
        total[:, cols(k)] = spread(own[:, cols(k)])

    def read(k):
        phase, here = k // chunks, k % chunks
        near_copy(k).wait_send()
        inner_copy(k).wait()
        outer_copy(k).wait()
        far_copy(k).wait()
        gather(land[phase, :, cols(here)], here)

        @pl.when(phase == 0)
        def _():
            own_spread(here)

        @pl.when(phase > 0)
        def _():
            total[:, cols(here)] += spread(land[jnp.maximum(phase - 1, 0), :, cols(here)])

        @pl.when(here == chunks - 1)
        def _():
            places = [
                block * occ_block + phase * occ_piece + i for block, _ in sources for i in range(occ_piece)]
            amplitude(occ_values(places) - vir_row[...])

    def arrive(k):
        near_copy(k).wait_recv()
        far_copy(k).start()

        @pl.when(k + AHEAD < steps)
        def _():
            send(k + AHEAD)

        @pl.when(k >= LAG)
        def _():
            read(k - LAG)

    every(steps, arrive)
    every(steps, read, steps - LAG)


def finish(total, land, amp_high, amp_low, out_ref, done, out_sem):
    amp = (amp_high[...], amp_low[...])
    chunks = total.shape[1] // CHUNK

    def store(k):
        return pltpu.make_async_copy(done.at[:, cols(k)], out_ref.at[:, cols(k)], out_sem.at[k])

    def tile(k):
        done[:, cols(k)] = total[:, cols(k)] + product(amp, split(land[STREAMS - 1, :, cols(k)]), (1, 0))
        store(k).start()

    every(chunks, tile)
    every(chunks, lambda k: store(k).wait())


def local(b_factors, occ_energy, vir_energy):
    occ_block, vir_block, width = b_factors.shape
    occ_count = lax.axis_size("occ")
    vir_count = lax.axis_size("vir")
    rows = occ_block * vir_block
    chunks = width // CHUNK
    steps = STREAMS * chunks
    block = pltpu.VMEM((rows, width), jnp.float32)
    half = pltpu.VMEM((rows, width), jnp.bfloat16)
    square = pltpu.VMEM((rows, rows), jnp.float32)
    vmem = pl.BlockSpec(memory_space=pltpu.VMEM)
    smem = pl.BlockSpec(memory_space=pltpu.SMEM)
    hbm = pl.BlockSpec(memory_space=pl.ANY)
    sems = [pltpu.SemaphoreType.DMA((count,)) for count in [chunks] + [steps] * 8]
    parts = pl.pallas_call(
        functools.partial(kernel, occ_count, vir_count, occ_block, vir_block),
        out_shape=[
            block,
            pltpu.VMEM((STREAMS, rows, width), jnp.float32),
            pltpu.VMEM((rows, rows), jnp.bfloat16),
            pltpu.VMEM((rows, rows), jnp.bfloat16),
        ],
        in_specs=[smem, smem, hbm],
        out_specs=[vmem] * 4,
        scratch_shapes=[block, half, half, square, square, pltpu.VMEM((8, rows), jnp.float32)] + sems,
        compiler_params=pltpu.CompilerParams(
            collective_id=0, has_side_effects=True, vmem_limit_bytes=42 * 2**20),
    )(occ_energy, vir_energy, b_factors.reshape(rows, width))
    out = pl.pallas_call(
        finish,
        out_shape=jax.ShapeDtypeStruct((rows, width), jnp.float32),
        in_specs=[vmem] * 4,
        out_specs=hbm,
        scratch_shapes=[block, pltpu.SemaphoreType.DMA((chunks,))],
        compiler_params=pltpu.CompilerParams(vmem_limit_bytes=10 * 2**20),
    )(*parts)
    return out.reshape(occ_block, vir_block, width)


def solution(mesh):
    in_specs = (P("occ", "vir", None), P(), P())
    out_specs = P("occ", "vir", None)
    return jax.shard_map(local, mesh=mesh, in_specs=in_specs, out_specs=out_specs, check_vma=False)
```

time: 120 us -> 109 us (0.908)
  Pallas kernels: 115 us -> 109 us
  local copies, waits for them, and re-layouts: 4.65 us -> 0 us
    pallas_call x1, Pallas kernels: 115 us -> 105 us  [local(): pl.pallas_call(functools.partial(kernel, occ_count, vir_count, occ_block,...]
    unnamed x1 -> x0, local copies, waits for them, and re-layouts: 4.65 us -> none
    pallas_call x0 -> x1, Pallas kernels: none -> 4.02 us  [local(): pl.pallas_call(finish, out_shape=jax.ShapeDtypeStruct((rows, width), jnp....]
where the time goes in v2:
time: 109 us
  Pallas kernels  109 us (100%)
    pallas_call x1, Pallas kernels, local(): pl.pallas_call(functools.partial(kernel, occ_count, vir_count, occ_block,...  105 us
    pallas_call x1, Pallas kernels, local(): pl.pallas_call(finish, out_shape=jax.ShapeDtypeStruct((rows, width), jnp....  4.02 us

profile of v2, /device:TPU:0, one launch (start us, length us, event | category | flops | bytes accessed | tf_op | source)
XLA Modules:
  0.0 108.7 jit_solution(11886499795241613453)
XLA Ops:
  0.0 104.7 %shard_map.37 = (f32[256,4096]{1,0:T(8,128)S(1)}, f32[4,256,4096]{2,1,0:T(8,128)S(1)}, bf16[256,256]{1,0:T(8,128)(2,1)S(1)}, bf16[256,256]{1,0:T(8,128)(2,1)S(1)}) custom-call(f32[32]{0:T(128)} %occ_ref.1, f32[256]{0:T(256)} %vir_ref.1, f32[256,4096]{1,0:T(8,128)} %bitcast.2), custom_call_target="tpu_custom_call" | custom-call | tf_op jit(solution)/shard_map/pallas_call | solution.py:221
  104.7 4.0 %shard_map.38 = f32[256,4096]{1,0:T(8,128)} custom-call(f32[256,4096]{1,0:T(8,128)S(1)} %get-tuple-element.9.total, f32[4,256,4096]{2,1,0:T(8,128)S(1)} %get-tuple-element.10.land, bf16[256,256]{1,0:T(8,128)(2,1)S(1)} %get-tuple-element.11.amp_high, bf16[256,256]{1,0:T(8,128)(2,1)S(1)} %get-tuple-element.12.amp_low), custom_call_target="tpu_custom_call" | custom-call | tf_op jit(solution)/shard_map/pallas_call | solution.py:235
